TPU v7x, 512 devices: a 8x2x16 block of a 8x8x16 slice. The times are simulated.
512 devices in a mesh: groups: 2 (over y), ctx: 32 (over z, core), tp: 8 (over x).
Axes of the slice: x: 8, y: 2, z: 16, core: 2. Of those that a mesh axis runs over, the one named last changes fastest.
The devices are a block of a 8x8x16 slice.
Arguments:
- query_matrix: bfloat16 [8192, 8192], P(('groups', 'ctx'), 'tp'), parts along dimension 0, may hold values from -20 to 20
- key_matrix: bfloat16 [8192, 1024], P(('groups', 'ctx'), 'tp'), parts along dimension 0, may hold values from -20 to 20
- value_matrix: bfloat16 [8192, 1024], P(('groups', 'ctx'), 'tp'), parts along dimension 0, may hold values from -6 to 6
- doc_ids: int32 [8192], P('groups'), parts along dimension 0, may hold values from 0 to 5, never falling along the last dimension, each value on 1 to 2048 neighbouring positions
- out_weight: bfloat16 [8192, 4096], P('tp', 'ctx'), may hold values from -0.0625 to 0.0625
Outputs:
- projected: bfloat16 [8192, 4096], P(('groups', 'ctx'), 'tp'), parts along dimension 0
There are 2 independent parts, one for each index of `groups`. A program takes and returns all parts, laid end to end along the dimension named above; an argument that names none is the same for every part. Nothing has to cross between parts.
Inputs may be any that keep to these rules, and one draw needn't show every extreme that they name: `doc_ids`: non-decreasing along the sequence; each document holds 1 to 2048 tokens, one exactly 2048.
All inputs are finite; a program needn't handle non-finite values.
Results may differ from a plain program's by a relative error of at most 0.015.
Values may be sent and summed in bfloat16 or wider, within the bound.
No kernel may reach another device: no remote copies, remote signals or barrier semaphores. Data moves between devices by JAX's collectives and lax.ppermute only.
A program may use at most 64 MiB of HBM per device.

v0:
```python
import math
import jax
import jax.numpy as jnp
from jax import lax
from jax.sharding import PartitionSpec as P

HEAD_SIZE = 128
rope_base = 1000000.0


def in_one_piece(arrays, axis, dim, along):
    ends, at = ([], 0)
    for a in arrays[:-1]:
        at += a.shape[along]
        ends.append(at)
    both = jnp.concatenate(arrays, axis=along)
    return tuple(jnp.split(lax.all_gather(both, axis, axis=dim, tiled=True), ends, axis=along))


def split_up(x, dim, size):
    lengths = x.shape
    pieces = x.reshape(*lengths[:dim], size, lengths[dim] // size, *lengths[dim + 1 :])
    return jnp.moveaxis(pieces, dim, 0)


def sent_and_summed(x, axis, dim):
    pieces = split_up(x, dim, lax.axis_size(axis))
    arrived = lax.all_to_all(pieces, axis, split_axis=0, concat_axis=0, tiled=True)
    return arrived.astype(jnp.float32).sum(axis=0)


def rotary_tables(rows, token_positions, heads):
    half_dim = HEAD_SIZE // 2
    frequency = jnp.power(
        jnp.float32(rope_base), -jnp.arange(half_dim, dtype=jnp.float32) * (2.0 / HEAD_SIZE)
    )
    angles = token_positions.astype(jnp.float32)[:, None] * frequency[None, :]
    cosine = jnp.cos(angles)[:, None, :]
    sine = jnp.sin(angles)[:, None, :]
    values = rows.astype(jnp.float32).reshape(rows.shape[0], heads, HEAD_SIZE)
    first = values[..., :half_dim]
    second = values[..., half_dim:]
    turned = jnp.concatenate([first * cosine - second * sine, second * cosine + first * sine], -1)
    return turned.reshape(rows.shape[0], heads * HEAD_SIZE).astype(jnp.bfloat16)


def keep_state(held_state, unused_block):
    return held_state


def on_device(query_matrix, key_matrix, value_matrix, doc_ids, out_weight):
    ctx_index = lax.axis_index("ctx")
    tok_rows = query_matrix.shape[0]
    query_heads = query_matrix.shape[1] // HEAD_SIZE
    key_heads = key_matrix.shape[1] // HEAD_SIZE
    group_width = query_heads // key_heads
    inverse_root = HEAD_SIZE ** (-0.5)
    local_rows = jnp.arange(tok_rows, dtype=jnp.int32)
    given_pos = ctx_index * tok_rows + local_rows
    query_matrix_rot = rotary_tables(query_matrix, given_pos, query_heads)
    keys_here = rotary_tables(key_matrix, given_pos, key_heads)
    query_doc = jnp.take(doc_ids, given_pos, axis=0)
    query_four = query_matrix_rot.reshape(tok_rows, key_heads, group_width, HEAD_SIZE)
    first_doc = jnp.min(query_doc)
    last_doc = jnp.max(query_doc)
    last_pos = jnp.max(given_pos)

    def attend(state, block):
        key_block, value_block, doc_block, pos_block = block
        row_max, totals, accum = state
        scores = (
            jnp.einsum("qkgd,skd->kgqs", query_four, key_block, preferred_element_type=jnp.float32)
            * inverse_root
        )
        allowed = (
            (query_doc[:, None] == doc_block[None, :]) & (pos_block[None, :] <= given_pos[:, None])
        )[None, None]
        new_max = jnp.maximum(row_max, jnp.max(jnp.where(allowed, scores, -1e30), -1))
        weights = jnp.where(allowed, jnp.exp(scores - new_max[..., None]), 0.0)
        factor = jnp.exp(row_max - new_max)
        totals = totals * factor + jnp.sum(weights, -1)
        accum = accum * jnp.transpose(factor, (2, 0, 1))[..., None] + jnp.einsum(
            "kgqs,skd->qkgd",
            weights.astype(jnp.bfloat16),
            value_block,
            preferred_element_type=jnp.float32,
        )
        return (new_max, totals, accum)

    start_state = (
        jnp.full((key_heads, group_width, tok_rows), -1e30, jnp.float32),
        jnp.zeros((key_heads, group_width, tok_rows), jnp.float32),
        jnp.zeros((tok_rows, key_heads, group_width, HEAD_SIZE), jnp.float32),
    )
    key_piece, value_piece = in_one_piece((keys_here, value_matrix), "ctx", 0, 1)
    count = key_piece.shape[0]
    block_rows = math.gcd(count, 512)
    block_count = count // block_rows
    positions = jnp.arange(count, dtype=jnp.int32)
    blocks = (
        key_piece.reshape(block_count, block_rows, key_heads, HEAD_SIZE),
        value_piece.reshape(block_count, block_rows, key_heads, HEAD_SIZE),
        jnp.take(doc_ids, positions, axis=0).reshape(block_count, block_rows),
        positions.reshape(block_count, block_rows),
    )

    def step_block(inner_state, block):
        live = (
            (jnp.min(block[3]) <= last_pos)
            & (jnp.min(block[2]) <= last_doc)
            & (jnp.max(block[2]) >= first_doc)
        )
        return (lax.cond(live, attend, keep_state, inner_state, block), None)

    final_state, unused_out = lax.scan(step_block, start_state, blocks)
    row_max, totals, accum = final_state
    attention = (
        (accum / jnp.transpose(totals, (2, 0, 1))[..., None])
        .reshape(tok_rows, query_heads * HEAD_SIZE)
        .astype(jnp.bfloat16)
    )
    terms = jnp.dot(
        attention,
        lax.all_gather(out_weight, "ctx", axis=1, tiled=True),
        preferred_element_type=jnp.float32,
    )
    return sent_and_summed(terms.astype(jnp.bfloat16), "tp", 1).astype(jnp.bfloat16)


def solution(mesh):
    in_specs = (
        P(("groups", "ctx"), "tp"),
        P(("groups", "ctx"), "tp"),
        P(("groups", "ctx"), "tp"),
        P("groups"),
        P("tp", "ctx"),
    )
    out_specs = P(("groups", "ctx"), "tp")
    return jax.shard_map(
        on_device, mesh=mesh, in_specs=in_specs, out_specs=out_specs, check_vma=False
    )
```

profile of v0, /device:TPU:65, one launch (start us, length us, event | category | flops | bytes accessed | tf_op | source)
XLA Modules:
  0.0 262.6 jit_solution(11426903617318993670)
XLA Ops:
  7.2 0.9 copy.19
  8.1 0.9 copy.20
  9.9 0.7 all-gather.5.cloned.1.call-update
  10.7 1.1 copy.21
  12.4 1.1 gather_fusion.1
  13.5 23.0 %gather_fusion = s32[4096]{0:T(1024)S(1)} fusion(s32[4096]{0:T(1024)S(1)} %copy-done, s32[4096]{0:T(1024)S(1)} %iota_clamp_fusion), kind=kCustom, calls=%fused_computation | custom fusion | bytes 49152 | tf_op jit(solution)/shard_map/jit(_take)/gather | solution.py:103
  36.6 0.7 fusion.39
  37.3 82.9 %all-gather.3.cloned.1.call-done = bf16[4096,256]{0,1:T(8,128)(2,1)} async-done(((bf16[128,256]{0,1:T(8,128)(2,1)}), bf16[4096,256]{0,1:T(8,128)(2,1)}) %all-gather.3.cloned.1.call-update) | async-done | bytes 2097168 | tf_op jit(solution)/shard_map/all_gather | solution.py:17
  120.2 1.7 fusion.41
  121.9 0.7 copy.22
  123.8 37.2 %while.15 = (s32[]{:T(128)}, f32[1,8,128]{2,1,0:T(8,128)S(1)}, f32[1,8,128]{2,1,0:T(8,128)S(1)}, f32[128,1,8,128]{0,3,2,1:T(8,128)S(1)}, s32[8,512]{1,0:T(8,128)...) while((s32[]{:T(128)}, f32[1,8,128]{2,1,0:T(8,128)S(1)}, ...), condition=%wide.region_11.12_spmd.clone, body=%wide.region_3.11_spmd.clone.sunk | while | flops 274666112 | bytes 8207207 | solution.py:115
  123.9 0.7 fusion.45
  128.2 1.8 conditional.3
  130.1 0.7 fusion.45
  134.5 0.7 fusion.45
  138.9 0.7 fusion.45
  143.3 0.7 fusion.45
  147.8 0.7 fusion.45
  152.2 0.7 fusion.45
  156.6 0.7 fusion.45
  161.1 54.5 %all-gather.5.cloned.1.call-done = bf16[1024,4096]{1,0:T(8,128)(2,1)} async-done(((bf16[1024,128]{1,0:T(8,128)(2,1)}), bf16[1024,4096]{1,0:T(8,128)(2,1)}) %all-gather.5.cloned.1.call-update) | async-done | bytes 8388624 | tf_op jit(solution)/shard_map/all_gather | solution.py:124
  215.6 4.7 %convolution_convert_fusion = bf16[128,4096]{1,0:T(8,128)(2,1)S(1)} fusion(bf16[128,1024]{0,1:T(8,128)(2,1)S(1)} %bitcast.90, bf16[1024,4096]{1,0:T(8,128)(2,1)} %all-gather.5.cloned.1.call-done), kind=kOutput, calls=%fused_computation.35 | convolution fusion | flops 1074266112 | bytes 9699328 | tf_op jit(solution)/shard_map/dot_general | solution.py:122
  220.3 34.6 %all_to_all.5 = bf16[8,128,512]{2,1,0:T(8,128)(2,1)S(1)} all-to-all(bf16[8,128,512]{2,1,0:T(8,128)(2,1)S(1)} %bitcast.85), channel_id=1, replica_groups=mesh['groups'=2,'ctx'=32,'tp'=8] {'tp'}, dimensions={0} | all-to-all | bytes 2097152 | tf_op jit(solution)/shard_map/all_to_all | solution.py:28
  254.9 0.8 reduce_sum.23
  (51 shorter events, 5.4 us)
Async XLA Ops:
  6.5 5.8 %copy-start = (s32[4096]{0:T(1024)S(1)}, s32[4096]{0:T(1024)}, u32[]{:S(2)}) copy-start(s32[4096]{0:T(1024)} %param.12) | copy-start | bytes 49156
  6.6 113.7 %all-gather.3.cloned.1.call-start = ((), (), s32[]{:S(2)}) async-start(), calls=%async_computation.1 | async-start | bytes 2162688 | tf_op jit(solution)/shard_map/all_gather | solution.py:17
  9.9 205.7 %all-gather.5.cloned.1.call-start = ((), (), s32[]{:S(2)}) async-start(), calls=%async_computation.2 | async-start | bytes 8650752 | tf_op jit(solution)/shard_map/all_gather | solution.py:124
Sparse Core Ops, SparseCore 0:
  10.0 110.2 all-gather.2
  122.3 93.2 all-gather.4
where the time goes:
time: 263 us
  waiting for transfers between devices  138 us (52%)
  blocking collectives  34.6 us (13%)
  local copies, waits for them, and re-layouts  30.9 us (12%)
  loops' own time  29.9 us (11%)
  between operations  13.6 us (5%)
  other arithmetic  9.57 us (4%)
  matrix products  5.76 us (2%)
    all_gather x1, waiting for transfers between devices, in_one_piece(): lax.all_gather(both, axis, axis=dim, tiled=True)  82.9 us
    all_gather x1, waiting for transfers between devices, on_device(): lax.all_gather(out_weight, 'ctx', axis=1, tiled=True)  54.5 us
    all_to_all x1, blocking collectives, sent_and_summed(): lax.all_to_all(pieces, axis, split_axis=0, concat_axis=0, tiled=True)  34.6 us
    another operation x1, loops' own time, on_device(): final_state, unused_out = lax.scan(step_block, start_state, blocks)  29.7 us
    gather x2, local copies, waits for them, and re-layouts, on_device(): jnp.take(doc_ids, positions, axis=0).reshape(block_count, block_rows)  23 us
    reduce_max x8, other arithmetic, step_block(): jnp.max(block[2]) >= first_doc  5.52 us
  transfers between devices with their start and end apart: 2, of which 2 were waited for; matrix products, arithmetic and copies ran while one was open for 14% of the time, Pallas kernels for 0%

commit v1 on v0

--- a/solution.py
+++ b/solution.py
@@ -6,6 +6,11 @@
 
 HEAD_SIZE = 128
 rope_base = 1000000.0
+
+
+def swapped_in(block, axis, along):
+    stack = jnp.stack([block] * lax.axis_size(axis))
+    return jnp.concatenate(lax.all_to_all(stack, axis, 0, 0), axis=along)
 
 
 def in_one_piece(arrays, axis, dim, along):
@@ -119,11 +124,7 @@
         .reshape(tok_rows, query_heads * HEAD_SIZE)
         .astype(jnp.bfloat16)
     )
-    terms = jnp.dot(
-        attention,
-        lax.all_gather(out_weight, "ctx", axis=1, tiled=True),
-        preferred_element_type=jnp.float32,
-    )
+    terms = jnp.dot(attention, swapped_in(out_weight, "ctx", 1), preferred_element_type=jnp.float32)
     return sent_and_summed(terms.astype(jnp.bfloat16), "tp", 1).astype(jnp.bfloat16)
 
 

time: 263 us -> 484 us (1.84); the launches traced: 263 us -> 477 us
  waiting for transfers between devices: 138 us -> 302 us
  starting transfers between devices: 0.07 us -> 46.3 us
    all_to_all x0 -> x1, waiting for transfers between devices: none -> 178 us  [swapped_in(): return jnp.concatenate(lax.all_to_all(stack, axis, 0, 0), axis=along)]
    all_gather x1 -> x0, waiting for transfers between devices: 54.5 us -> none  [on_device(): lax.all_gather(out_weight, 'ctx', axis=1, tiled=True)]
    all_to_all x0 -> x1, starting transfers between devices: none -> 46.3 us  [swapped_in(): return jnp.concatenate(lax.all_to_all(stack, axis, 0, 0), axis=along)]
    all_gather x1, waiting for transfers between devices: 82.9 us -> 125 us  [in_one_piece(): lax.all_gather(both, axis, axis=dim, tiled=True)]
  transfers between devices with their start and end apart: 2 -> 2, of which waited for: 2 -> 2; matrix products, arithmetic and copies ran while one was open for 14% -> 8% of each run, Pallas kernels for 0% -> 0%
where the time goes in v1:
time: 484 us; the launch traced here: 477 us
  waiting for transfers between devices  302 us (62%)
  starting transfers between devices  46.3 us (10%)
  local copies, waits for them, and re-layouts  33.8 us (7%)
  blocking collectives  33.7 us (7%)
  loops' own time  29.5 us (6%)
  between operations  13.7 us (3%)
  other arithmetic  9.82 us (2%)
  matrix products  7.38 us (2%)
    all_to_all x1, waiting for transfers between devices, swapped_in(): return jnp.concatenate(lax.all_to_all(stack, axis, 0, 0), axis=along)  178 us
    all_gather x1, waiting for transfers between devices, in_one_piece(): lax.all_gather(both, axis, axis=dim, tiled=True)  125 us
    all_to_all x1, starting transfers between devices, swapped_in(): return jnp.concatenate(lax.all_to_all(stack, axis, 0, 0), axis=along)  46.3 us
    all_to_all x1, blocking collectives, sent_and_summed(): lax.all_to_all(pieces, axis, split_axis=0, concat_axis=0, tiled=True)  33.7 us
    another operation x1, loops' own time, on_device(): final_state, unused_out = lax.scan(step_block, start_state, blocks)  29.4 us
    gather x2, local copies, waits for them, and re-layouts, on_device(): jnp.take(doc_ids, positions, axis=0).reshape(block_count, block_rows)  23 us
  transfers between devices with their start and end apart: 2, of which 2 were waited for; matrix products, arithmetic and copies ran while one was open for 8% of the time, Pallas kernels for 0%

profile of v1, /device:TPU:65, one launch (start us, length us, event | category | flops | bytes accessed | tf_op | source)
XLA Modules:
  0.0 476.6 jit_solution(9979901134041676084)
XLA Ops:
  6.6 1.1 copy.28
  7.7 4.3 stack.2
  11.9 46.3 %all-to-all-start = ((bf16[32,1024,128]{1,2,0:T(8,128)(2,1)}), bf16[32,1024,128]{1,2,0:T(8,128)(2,1)}, u32[]{:S(2)}, u32[]{:S(2)}) async-start(bf16[32,1024,128]{1,2,0:T(8,128)(2,1)} %stack.2), calls=%async_computation | async-start | bytes 16777216 | tf_op jit(solution)/shard_map/all_to_all | solution.py:13
  60.2 1.1 gather_fusion.1
  61.4 23.0 %gather_fusion = s32[4096]{0:T(1024)S(1)} fusion(s32[4096]{0:T(1024)S(1)} %copy-done, s32[4096]{0:T(1024)S(1)} %iota_clamp_fusion), kind=kCustom, calls=%fused_computation | custom fusion | bytes 49152 | tf_op jit(solution)/shard_map/jit(_take)/gather | solution.py:108
  85.1 0.6 fusion.39
  85.8 124.6 %all-gather.2.cloned.1.call-done = bf16[4096,256]{0,1:T(8,128)(2,1)} async-done(((bf16[128,256]{0,1:T(8,128)(2,1)}), bf16[4096,256]{0,1:T(8,128)(2,1)}) %all-gather.2.cloned.1.call-update) | async-done | bytes 2097168 | tf_op jit(solution)/shard_map/all_gather | solution.py:22
  210.4 1.7 fusion.41
  212.1 0.7 copy.24
  213.3 0.7 copy.31
  214.0 37.1 %while.15 = (s32[]{:T(128)}, f32[1,8,128]{2,1,0:T(8,128)S(1)}, f32[1,8,128]{2,1,0:T(8,128)S(1)}, f32[128,1,8,128]{0,3,2,1:T(8,128)S(1)}, s32[8,512]{1,0:T(8,128)...) while((s32[]{:T(128)}, f32[1,8,128]{2,1,0:T(8,128)S(1)}, ...), condition=%wide.region_11.12_spmd.clone, body=%wide.region_3.11_spmd.clone.sunk | while | flops 274666112 | bytes 8207215 | solution.py:120
  214.1 0.7 fusion.45
  218.4 1.8 conditional.3
  220.3 0.7 fusion.45
  224.7 0.7 fusion.45
  229.1 0.7 fusion.45
  233.5 0.7 fusion.45
  237.9 0.7 fusion.45
  242.4 0.7 fusion.45
  246.8 0.7 fusion.45
  251.2 177.6 %all-to-all-done = bf16[32,1024,128]{1,2,0:T(8,128)(2,1)} async-done(((bf16[32,1024,128]{1,2,0:T(8,128)(2,1)}), bf16[32,1024,128]{1,2,0:T(8,128)(2,1)}, u32[]{:S(2)}, u32[]{:S(2)}) %all-to-all-start) | async-done | bytes 8388640 | tf_op jit(solution)/shard_map/all_to_all | solution.py:13
  428.9 6.3 %convolution_convert_fusion = bf16[128,4096]{1,0:T(8,128)(2,1)S(1)} fusion(bf16[128,1024]{0,1:T(8,128)(2,1)S(1)} %bitcast.93, bf16[1024,4096]{0,1:T(8,128)(2,1)} %bitcast.32), kind=kOutput, calls=%fused_computation.35 | convolution fusion | flops 1074266112 | bytes 9699328 | tf_op jit(solution)/shard_map/dot_general | solution.py:127
  435.2 33.7 %all_to_all.10 = bf16[8,128,512]{2,1,0:T(8,128)(2,1)S(1)} all-to-all(bf16[8,128,512]{2,1,0:T(8,128)(2,1)S(1)} %bitcast.89), channel_id=1, replica_groups=mesh['groups'=2,'ctx'=32,'tp'=8] {'tp'}, dimensions={0} | all-to-all | bytes 2097152 | tf_op jit(solution)/shard_map/all_to_all | solution.py:33
  468.9 0.8 reduce_sum.23
  (58 shorter events, 5.1 us)
Async XLA Ops:
  6.5 53.6 %copy-start = (s32[4096]{0:T(1024)S(1)}, s32[4096]{0:T(1024)}, u32[]{:S(2)}) copy-start(s32[4096]{0:T(1024)} %param.12) | copy-start | bytes 49156
  11.9 46.4 %copy-start.2 = (bf16[128,128]{1,0:T(8,128)(2,1)S(1)}, bf16[128,128]{1,0:T(8,128)(2,1)}, u32[]{:S(2)}) copy-start(bf16[128,128]{1,0:T(8,128)(2,1)} %param.10) | copy-start | bytes 98308
  11.9 46.5 %copy-start.3 = (bf16[128,128]{1,0:T(8,128)(2,1)S(1)}, bf16[128,128]{1,0:T(8,128)(2,1)}, u32[]{:S(2)}) copy-start(bf16[128,128]{1,0:T(8,128)(2,1)} %param.11) | copy-start | bytes 98308
  11.9 416.9 %all-to-all-start = ((bf16[32,1024,128]{1,2,0:T(8,128)(2,1)}), bf16[32,1024,128]{1,2,0:T(8,128)(2,1)}, u32[]{:S(2)}, u32[]{:S(2)}) async-start(bf16[32,1024,128]{1,2,0:T(8,128)(2,1)} %stack.2), calls=%async_computation | async-start | bytes 16777216 | tf_op jit(solution)/shard_map/all_to_all | solution.py:13
  58.2 152.2 %all-gather.2.cloned.1.call-start = ((), (), s32[]{:S(2)}) async-start(), calls=%async_computation.2 | async-start | bytes 2162688 | tf_op jit(solution)/shard_map/all_gather | solution.py:22
  61.4 23.1 %copy-start.1 = (bf16[128,1024]{1,0:T(8,128)(2,1)S(1)}, bf16[128,1024]{1,0:T(8,128)(2,1)}, u32[]{:S(2)}) copy-start(bf16[128,1024]{1,0:T(8,128)(2,1)} %param.9) | copy-start | bytes 786436
Sparse Core Ops, SparseCore 0:
  61.1 149.2 all-gather.1
